TPU v7x, 32 devices: a whole 2x2x4 slice. The times are simulated.
32 devices in a mesh: path: 8 (over z, core), tm: 4 (over y, x).
Axes of the slice: x: 2, y: 2, z: 4, core: 2. Of those that a mesh axis runs over, the one named last changes fastest.
Arguments:
- shock_rate: float32 [64, 131072], P('tm', 'path'), may hold values from -6 to 6
- shock_fx: float32 [4, 64, 131072], P(None, 'tm', 'path'), may hold values from -6 to 6
- fx_vol: float32 [4], replicated, may hold values from 0.1 to 0.4
- fx_corr: float32 [4], replicated, may hold values from -0.8 to 0.8
- hazard_scale: float32 [32], replicated, may hold values from 0.03 to 3
- counterparty: int32 [512], replicated, may hold values from 0 to 31
- currency: int32 [512], replicated, may hold values from 0 to 3
- maturity: int32 [512], replicated, may hold values from 1 to 64
- notional: float32 [512], replicated, may hold values from -8 to 8
- strike: float32 [512], replicated, may hold values from 0.7 to 1.3
Outputs:
- profile: float32 [64, 32], P('tm')
- cva: float32 [32], replicated
All inputs are finite; a program needn't handle non-finite values.
Results may differ from a plain program's by a relative error of at most 0.000061.
Values sent between devices are 32-bit elements; how exact they have to be, the bound alone decides.
A program may use at most 64 MiB of HBM per device.

v0:
```python
import math
import jax
import jax.numpy as jnp
from jax import lax
from jax.sharding import PartitionSpec as P

HORIZON = 5.0
RATE_DOM = 0.03
RATE_FOR = 0.01
LOSS_SHARE = 0.6
RATE_SHIFT = 1.5
HIGHEST_PREC = lax.Precision.HIGHEST


def carried_in(part, axis, combine, identity):
    place = lax.axis_index(axis)
    gathered = jax.tree.map(lambda a: lax.all_gather(a, axis), part)
    state = jax.tree.map(lambda a, e: jnp.zeros_like(a) + jnp.asarray(e, a.dtype), part, identity)

    def one(turn, state):
        return combine(
            state, jax.tree.map(lambda a: lax.dynamic_index_in_dim(a, turn, 0, False), gathered)
        )

    return lax.fori_loop(0, place, one, state)


def trade_tables(
    date_rows, counterparty, currency, maturity, notional, strike, cp_count, ccy_count, date_step
):
    is_alive = (date_rows[:, None] < maturity[None, :]).astype(jnp.float32)
    time_left = (maturity[None, :] - date_rows[:, None]).astype(jnp.float32) * date_step
    weight_for = is_alive * notional[None, :] * jnp.exp(-RATE_FOR * time_left)
    weight_dom = is_alive * (notional * strike)[None, :] * jnp.exp(-RATE_DOM * time_left)
    member = (counterparty[None, :] == jnp.arange(cp_count, dtype=jnp.int32)[:, None]).astype(
        jnp.float32
    )
    currency_onehot = (currency[None, :] == jnp.arange(ccy_count, dtype=jnp.int32)[:, None]).astype(
        jnp.float32
    )
    fwd_table = jnp.einsum(
        "ck,tk,jk->tcj", member, weight_for, currency_onehot, precision=HIGHEST_PREC
    )
    dom_table = jnp.einsum("ck,tk->tc", member, weight_dom, precision=HIGHEST_PREC)
    return (fwd_table, dom_table)


def weigh_block(block_item, hazard_scale):
    fwd_table, dom_table, spot, hazard_prev, hazard_cur = block_item
    netted = (
        jnp.einsum("tcj,tjp->tcp", fwd_table, spot, precision=HIGHEST_PREC) - dom_table[:, :, None]
    )
    exposure = jnp.maximum(netted, 0.0)
    scale_row = hazard_scale[None, :, None]
    density = jnp.exp(-scale_row * hazard_prev[:, None, :]) - jnp.exp(
        -scale_row * hazard_cur[:, None, :]
    )
    return jnp.sum(exposure * density, axis=2)


def weigh_dates(fwd_table, dom_table, spot, hazard_prev, hazard_cur, hazard_scale):
    date_count, path_count = hazard_cur.shape
    cp_count = dom_table.shape[1]
    ccy_count = spot.shape[1]
    block_dates = math.gcd(date_count, max(1, 32768 // path_count))
    groups = date_count // block_dates
    blocks = (
        fwd_table.reshape(groups, block_dates, cp_count, ccy_count),
        dom_table.reshape(groups, block_dates, cp_count),
        spot.reshape(groups, block_dates, ccy_count, path_count),
        hazard_prev.reshape(groups, block_dates, path_count),
        hazard_cur.reshape(groups, block_dates, path_count),
    )
    weighed = lax.map(lambda block_item: weigh_block(block_item, hazard_scale), blocks)
    return weighed.reshape(date_count, cp_count)


def local_walk(rate_shock, other_shock, fx_vol, fx_corr, date_step, decay_rate, noise_scale):
    date_count = rate_shock.shape[0]
    date_index = jnp.arange(date_count, dtype=jnp.int32)
    date_gap = date_index[:, None] - date_index[None, :]
    is_below = date_gap >= 0
    powers = jnp.where(is_below, decay_rate ** jnp.maximum(date_gap, 0).astype(jnp.float32), 0.0)
    lower_ones = is_below.astype(jnp.float32)
    rate_walk = noise_scale * jnp.dot(powers, rate_shock, precision=HIGHEST_PREC)
    mix_weight = jnp.sqrt(1.0 - fx_corr * fx_corr)
    mixed = fx_corr[:, None, None] * rate_shock[None] + mix_weight[:, None, None] * other_shock
    moves = (fx_vol * math.sqrt(date_step))[:, None, None] * mixed - (
        0.5 * fx_vol * fx_vol * date_step
    )[:, None, None]
    fx_walk = jnp.einsum("ts,jsp->tjp", lower_ones, moves, precision=HIGHEST_PREC)
    carry_gain = decay_rate ** (jnp.arange(date_count, dtype=jnp.float32) + 1.0)
    return (rate_walk, fx_walk, carry_gain, lower_ones)


def path_intensity(rate_walk, carry_gain, rate_in):
    shifted = rate_walk + carry_gain[:, None] * rate_in[None, :] + RATE_SHIFT
    return 0.1 + 0.5 * shifted * shifted


def finish_paths(intensity, lower_ones, fx_walk, hazard_in, log_in, date_step):
    hazard_cur = hazard_in[None, :] + date_step * jnp.dot(
        lower_ones, intensity, precision=HIGHEST_PREC
    )
    hazard_prev = hazard_cur - date_step * intensity
    spot = jnp.exp(fx_walk + log_in[None])
    return (hazard_prev, hazard_cur, spot)


def combine_affine(earlier, later):
    gain_a, end_a, log_a = earlier
    gain_b, end_b, log_b = later
    return (gain_b * gain_a, gain_b * end_a + end_b, log_a + log_b)


def combine_total(earlier, later):
    return earlier + later


def per_device(
    shock_rate,
    shock_fx,
    fx_vol,
    fx_corr,
    hazard_scale,
    counterparty,
    currency,
    maturity,
    notional,
    strike,
):
    local_dates = shock_rate.shape[0]
    total_dates = local_dates * lax.axis_size("tm")
    total_paths = shock_rate.shape[1] * lax.axis_size("path")
    cp_count = hazard_scale.shape[0]
    ccy_count = fx_vol.shape[0]
    date_step = HORIZON / total_dates
    decay_rate = math.exp(-2.0 / total_dates)
    noise_scale = math.sqrt(1.0 - decay_rate * decay_rate)
    first_date = lax.axis_index("tm") * local_dates
    rate_walk, fx_walk, carry_gain, lower_ones = local_walk(
        shock_rate, shock_fx, fx_vol, fx_corr, date_step, decay_rate, noise_scale
    )
    blank = jnp.zeros_like(rate_walk[0])
    span_gain = jnp.full((1,), decay_rate**local_dates, jnp.float32)
    unit_gain = jnp.ones((1,), jnp.float32)
    log_blank = jnp.zeros_like(fx_walk[0])
    carried = carried_in(
        (span_gain, rate_walk[-1], fx_walk[-1]), "tm", combine_affine, (unit_gain, blank, log_blank)
    )
    rate_in, log_in = (carried[1], carried[2])
    intensity = path_intensity(rate_walk, carry_gain, rate_in)
    block_total = date_step * jnp.sum(intensity, axis=0)
    hazard_in = carried_in(block_total, "tm", combine_total, blank)
    hazard_prev, hazard_cur, spot = finish_paths(
        intensity, lower_ones, fx_walk, hazard_in, log_in, date_step
    )
    date_rows = first_date + jnp.arange(local_dates, dtype=jnp.int32)
    fwd_table, dom_table = trade_tables(
        date_rows,
        counterparty,
        currency,
        maturity,
        notional,
        strike,
        cp_count,
        ccy_count,
        date_step,
    )
    local_sum = weigh_dates(fwd_table, dom_table, spot, hazard_prev, hazard_cur, hazard_scale)
    discount = jnp.exp(-RATE_DOM * date_step * (jnp.arange(total_dates, dtype=jnp.float32) + 1.0))
    profile = lax.psum(local_sum, "path") / (total_paths * date_step)
    own_discount = lax.dynamic_slice_in_dim(discount, first_date, local_dates, 0)
    cva = lax.psum(LOSS_SHARE * date_step * jnp.sum(own_discount[:, None] * profile, axis=0), "tm")
    return (profile, cva)


def solution(mesh):
    return jax.shard_map(
        per_device,
        mesh=mesh,
        in_specs=(P("tm", "path"), P(None, "tm", "path"), P(), P(), P(), P(), P(), P(), P(), P()),
        out_specs=(P("tm", None), P()),
        check_vma=False,
    )
```

profile of v0, /device:TPU:0, one launch (start us, length us, event | category | flops | bytes accessed | tf_op | source)
XLA Modules:
  0.0 156.9 jit_solution(9286434855395764987)
XLA Ops:
  7.2 0.7 broadcast_multiply_fusion.3
  7.9 5.5 %fusion.8 = f32[16,4,16384]{2,0,1:T(8,128)S(1)} fusion(f32[4,16,16384]{2,1,0:T(8,128)} %param.17, f32[4]{0:T(128)S(1)} %get-tuple-element.248, f32[4]{0:T(128)S(1)} %get-tuple-element.251, f32[16,16384]{1,0:T(8,128)} %param.16, f32[4]{0:T(128)} %param.19, f32[4]{0:T(128)S(1)} %get-tuple-element.247), kind=kOutput, calls=%fused_computation.23 | convolution fusion | flops 206569984 | bytes 9437248 | tf_op jit(solution)/shard_map/ts,jsp->tjp/dot_general | solution.py:91
  13.4 1.9 %copy-done = f32[16,4,16384]{2,0,1:T(8,128)} copy-done((f32[16,4,16384]{2,0,1:T(8,128)}, f32[16,4,16384]{2,0,1:T(8,128)S(1)}, u32[]{:S(2)}) %copy-start) | copy-done | bytes 4194328
  15.4 0.2 slice.9
  15.6 0.9 copy.15
  16.6 1.0 convolution_multiply_fusion.1
  17.6 10.5 %all-gather.1 = f32[4,1,16384]{2,1,0:T(1,128)S(1)} all-gather(f32[1,1,16384]{2,1,0:T(1,128)S(1)} %slice_bitcast_fusion), channel_id=1, replica_groups=mesh['path'=8,'tm'=4] {'tm'}, dimensions={0}, use_global_device_ids=true | all-gather | bytes 327680 | tf_op jit(solution)/shard_map/all_gather | solution.py:17
  28.1 0.6 dynamic-slice
  28.7 0.8 dynamic-update-slice
  29.5 8.9 %all-reduce = f32[4]{0:T(128)S(1)} all-reduce(f32[4]{0:T(128)S(1)} %dynamic-update-slice), channel_id=1, replica_groups=mesh['path'=8,'tm'=4] {'tm'}, use_global_device_ids=true, to_apply=%add | all-reduce | flops 4 | bytes 32
  38.8 0.2 fusion.23
  39.1 0.2 fusion.20
  39.3 6.6 %all-gather.4.cloned.1.call-done = f32[4,4,16384]{2,1,0:T(4,128)} async-done(((f32[1,4,16384]{2,1,0:T(4,128)}), f32[4,4,16384]{2,1,0:T(4,128)}) %all-gather.4.cloned.1.call-update) | async-done | bytes 1048592 | tf_op jit(solution)/shard_map/all_gather | solution.py:17
  46.0 2.7 %add_exponential_fusion = f32[16,4,16384]{2,0,1:T(8,128)S(1)} fusion(f32[16,4,16384]{2,0,1:T(8,128)} %copy-done, f32[4,16384]{1,0:T(4,128)S(1)} %get-tuple-element.178), kind=kLoop, calls=%fused_computation.22 | loop fusion | flops 1048576 | bytes 8650752 | tf_op jit(solution)/shard_map/exp | solution.py:106
  48.7 4.6 %copy.18 = f32[16,4,16384]{2,1,0:T(4,128)} copy(f32[16,4,16384]{2,0,1:T(8,128)S(1)} %add_exponential_fusion) | data formatting | bytes 8388608 | tf_op jit(solution)/shard_map/while | solution.py:74
  53.4 0.4 fusion.66
  53.8 15.0 %all-gather = f32[65536]{0:T(1024)S(1)} all-gather(f32[16384]{0:T(1024)S(1)} %broadcast_multiply_fusion), channel_id=2, replica_groups=mesh['path'=8,'tm'=4] {'tm'}, dimensions={0}, use_global_device_ids=true | all-gather | bytes 327680 | tf_op jit(solution)/shard_map/all_gather | solution.py:17
  69.1 2.1 %multiply_subtract_fusion = (f32[16,16384]{1,0:T(8,128)}, f32[16,16384]{1,0:T(8,128)S(1)}) fusion(f32[16,16384]{1,0:T(8,128)S(1)} %convolution_multiply_fusion.1, f32[16384]{0:T(1024)S(1)} %get-tuple-element.179, f32[16]{0:T(128)S(1)} %add_power_fusion, f32[16384]{0:T(1024)S(1)} %get-tuple-element.180), kind=kOutput, calls=%fused_computation.36 | convolution fusion | flops 54526464 | bytes 3276864 | tf_op jit(solution)/shard_map/dot_general | solution.py:102
  71.2 1.8 %reshape.69 = f32[8,2,16384]{2,1,0:T(2,128)S(1)} reshape(f32[16,16384]{1,0:T(8,128)} %get-tuple-element.249) | data formatting | bytes 2097152 | tf_op jit(solution)/shard_map/reshape | solution.py:71
  73.1 0.6 reshape.70
  73.7 51.0 %while.38 = (s32[]{:T(128)}, f32[8,2,32]{2,1,0:T(2,128)S(1)}, f32[8,2,32,4]{2,1,0,3:T(2,128)S(1)}, f32[8,2,4,16384]{3,2,1,0:T(4,128)}, f32[8,2,32]{2,1,0:T(2,128...) while((s32[]{:T(128)}, f32[8,2,32]{2,1,0:T(2,128)S(1)}, ...), condition=%wide.region_7.8_spmd, body=%wide.region_5.7_spmd.sunk | while | flops 57671616 | bytes 1317113 | solution.py:74
  73.8 6.3 %fusion.73 = f32[2,32]{1,0:T(2,128)S(1)} fusion(f32[2,16384]{1,0:T(2,128)S(1)} %get-tuple-element.373, f32[2,16384]{1,0:T(2,128)S(1)} %get-tuple-element.374, f32[32]{0:T(128)S(1)} %bitcast.77, f32[2,32]{1,0:T(2,128)S(1)} %fusion.72, f32[8,2,4,16384]{3,2,1,0:T(4,128)} %get-tuple-element.447, s32[]{:T(128)S(6)} %copy.46, ...), kind=kOutput, calls=%fused_computation.8.clone.1 | convolution fusion | flops 57671616 | bytes 788100 | tf_op jit(solution)/shard_map/while/body/eval_jaxpr/tcj,tjp->tcp/dot_general | solution.py:51
  80.1 6.3 %fusion.73 = f32[2,32]{1,0:T(2,128)S(1)} fusion(f32[2,16384]{1,0:T(2,128)S(1)} %get-tuple-element.373, f32[2,16384]{1,0:T(2,128)S(1)} %get-tuple-element.374, f32[32]{0:T(128)S(1)} %bitcast.77, f32[2,32]{1,0:T(2,128)S(1)} %fusion.72, f32[8,2,4,16384]{3,2,1,0:T(4,128)} %get-tuple-element.447, s32[]{:T(128)S(6)} %copy.46, ...), kind=kOutput, calls=%fused_computation.8.clone.1 | convolution fusion | flops 57671616 | bytes 788100 | tf_op jit(solution)/shard_map/while/body/eval_jaxpr/tcj,tjp->tcp/dot_general | solution.py:51
  86.5 6.3 %fusion.73 = f32[2,32]{1,0:T(2,128)S(1)} fusion(f32[2,16384]{1,0:T(2,128)S(1)} %get-tuple-element.373, f32[2,16384]{1,0:T(2,128)S(1)} %get-tuple-element.374, f32[32]{0:T(128)S(1)} %bitcast.77, f32[2,32]{1,0:T(2,128)S(1)} %fusion.72, f32[8,2,4,16384]{3,2,1,0:T(4,128)} %get-tuple-element.447, s32[]{:T(128)S(6)} %copy.46, ...), kind=kOutput, calls=%fused_computation.8.clone.1 | convolution fusion | flops 57671616 | bytes 788100 | tf_op jit(solution)/shard_map/while/body/eval_jaxpr/tcj,tjp->tcp/dot_general | solution.py:51
  92.9 6.3 %fusion.73 = f32[2,32]{1,0:T(2,128)S(1)} fusion(f32[2,16384]{1,0:T(2,128)S(1)} %get-tuple-element.373, f32[2,16384]{1,0:T(2,128)S(1)} %get-tuple-element.374, f32[32]{0:T(128)S(1)} %bitcast.77, f32[2,32]{1,0:T(2,128)S(1)} %fusion.72, f32[8,2,4,16384]{3,2,1,0:T(4,128)} %get-tuple-element.447, s32[]{:T(128)S(6)} %copy.46, ...), kind=kOutput, calls=%fused_computation.8.clone.1 | convolution fusion | flops 57671616 | bytes 788100 | tf_op jit(solution)/shard_map/while/body/eval_jaxpr/tcj,tjp->tcp/dot_general | solution.py:51
  99.2 6.3 %fusion.73 = f32[2,32]{1,0:T(2,128)S(1)} fusion(f32[2,16384]{1,0:T(2,128)S(1)} %get-tuple-element.373, f32[2,16384]{1,0:T(2,128)S(1)} %get-tuple-element.374, f32[32]{0:T(128)S(1)} %bitcast.77, f32[2,32]{1,0:T(2,128)S(1)} %fusion.72, f32[8,2,4,16384]{3,2,1,0:T(4,128)} %get-tuple-element.447, s32[]{:T(128)S(6)} %copy.46, ...), kind=kOutput, calls=%fused_computation.8.clone.1 | convolution fusion | flops 57671616 | bytes 788100 | tf_op jit(solution)/shard_map/while/body/eval_jaxpr/tcj,tjp->tcp/dot_general | solution.py:51
  105.6 6.3 %fusion.73 = f32[2,32]{1,0:T(2,128)S(1)} fusion(f32[2,16384]{1,0:T(2,128)S(1)} %get-tuple-element.373, f32[2,16384]{1,0:T(2,128)S(1)} %get-tuple-element.374, f32[32]{0:T(128)S(1)} %bitcast.77, f32[2,32]{1,0:T(2,128)S(1)} %fusion.72, f32[8,2,4,16384]{3,2,1,0:T(4,128)} %get-tuple-element.447, s32[]{:T(128)S(6)} %copy.46, ...), kind=kOutput, calls=%fused_computation.8.clone.1 | convolution fusion | flops 57671616 | bytes 788100 | tf_op jit(solution)/shard_map/while/body/eval_jaxpr/tcj,tjp->tcp/dot_general | solution.py:51
  112.0 6.3 %fusion.73 = f32[2,32]{1,0:T(2,128)S(1)} fusion(f32[2,16384]{1,0:T(2,128)S(1)} %get-tuple-element.373, f32[2,16384]{1,0:T(2,128)S(1)} %get-tuple-element.374, f32[32]{0:T(128)S(1)} %bitcast.77, f32[2,32]{1,0:T(2,128)S(1)} %fusion.72, f32[8,2,4,16384]{3,2,1,0:T(4,128)} %get-tuple-element.447, s32[]{:T(128)S(6)} %copy.46, ...), kind=kOutput, calls=%fused_computation.8.clone.1 | convolution fusion | flops 57671616 | bytes 788100 | tf_op jit(solution)/shard_map/while/body/eval_jaxpr/tcj,tjp->tcp/dot_general | solution.py:51
  118.3 6.3 %fusion.73 = f32[2,32]{1,0:T(2,128)S(1)} fusion(f32[2,16384]{1,0:T(2,128)S(1)} %get-tuple-element.373, f32[2,16384]{1,0:T(2,128)S(1)} %get-tuple-element.374, f32[32]{0:T(128)S(1)} %bitcast.77, f32[2,32]{1,0:T(2,128)S(1)} %fusion.72, f32[8,2,4,16384]{3,2,1,0:T(4,128)} %get-tuple-element.447, s32[]{:T(128)S(6)} %copy.46, ...), kind=kOutput, calls=%fused_computation.8.clone.1 | convolution fusion | flops 57671616 | bytes 788100 | tf_op jit(solution)/shard_map/while/body/eval_jaxpr/tcj,tjp->tcp/dot_general | solution.py:51
  124.7 15.0 %psum.14 = f32[16,32]{1,0:T(8,128)S(1)} all-reduce(f32[16,32]{1,0:T(8,128)S(1)} %bitcast.74), channel_id=1, replica_groups=mesh['path'=8,'tm'=4] {'path'}, use_global_device_ids=true, to_apply=%region_8.9 | all-reduce | flops 512 | bytes 4096 | tf_op jit(solution)/shard_map/psum | solution.py:172
  139.7 0.6 multiply_reduce_fusion
  140.3 9.7 %psum.15 = f32[32]{0:T(128)} all-reduce(f32[32]{0:T(128)S(1)} %broadcast_multiply_fusion.2), channel_id=1, replica_groups=mesh['path'=8,'tm'=4] {'tm'}, use_global_device_ids=true, to_apply=%region_10.11 | all-reduce | flops 32 | bytes 256 | tf_op jit(solution)/shard_map/psum | solution.py:174
  (71 shorter events, 1.3 us)
Async XLA Ops:
  7.2 38.8 %all-gather.4.cloned.1.call-start = ((), (), s32[]{:S(2)}) async-start(), calls=%async_computation | async-start | bytes 1310720 | tf_op jit(solution)/shard_map/all_gather | solution.py:17
  7.9 8.7 %copy-start.1 = (f32[16,16384]{1,0:T(8,128)S(1)}, f32[16,16384]{1,0:T(8,128)}, u32[]{:S(2)}) copy-start(f32[16,16384]{1,0:T(8,128)} %param.16) | copy-start | bytes 3145732
  7.9 20.2 %copy-start.8 = (u32[32]{0:T(128)S(1)}, u32[32]{0:T(128)}, u32[]{:S(2)}) copy-start(u32[32]{0:T(128)} %constant.112) | copy-start | bytes 388
  13.4 1.9 %copy-start = (f32[16,4,16384]{2,0,1:T(8,128)}, f32[16,4,16384]{2,0,1:T(8,128)S(1)}, u32[]{:S(2)}) copy-start(f32[16,4,16384]{2,0,1:T(8,128)S(1)} %fusion.8) | copy-start | bytes 12582916
  15.4 23.2 %copy-start.2 = (f32[512]{0:T(512)S(1)}, f32[512]{0:T(512)}, u32[]{:S(2)}) copy-start(f32[512]{0:T(512)} %param.24) | copy-start | bytes 6148
  15.4 23.2 %copy-start.3 = (f32[512]{0:T(512)S(1)}, f32[512]{0:T(512)}, u32[]{:S(2)}) copy-start(f32[512]{0:T(512)} %param.25) | copy-start | bytes 6148
  15.4 23.4 %copy-start.7 = (f32[32]{0:T(128)S(1)}, f32[32]{0:T(128)}, u32[]{:S(2)}) copy-start(f32[32]{0:T(128)} %param.20) | copy-start | bytes 388
  15.4 23.4 %copy-start.4 = (s32[512]{0:T(512)S(1)}, s32[512]{0:T(512)}, u32[]{:S(2)}) copy-start(s32[512]{0:T(512)} %param.22) | copy-start | bytes 6148
  15.4 23.4 %copy-start.5 = (s32[512]{0:T(512)S(1)}, s32[512]{0:T(512)}, u32[]{:S(2)}) copy-start(s32[512]{0:T(512)} %param.23) | copy-start | bytes 6148
  15.4 23.4 %copy-start.6 = (s32[512]{0:T(512)S(1)}, s32[512]{0:T(512)}, u32[]{:S(2)}) copy-start(s32[512]{0:T(512)} %param.21) | copy-start | bytes 6148
Sparse Core Ops, SparseCore 0:
  16.7 29.2 all-gather.3
where the time goes:
time: 157 us
  matrix products  59.4 us (38%)
  blocking collectives  59.1 us (38%)
  between operations  14.3 us (9%)
  local copies, waits for them, and re-layouts  12.3 us (8%)
  waiting for transfers between devices  6.65 us (4%)
  other arithmetic  4.69 us (3%)
    dot_general x8, matrix products, weigh_block(): jnp.einsum('tcj,tjp->tcp', fwd_table, spot, precision=HIGHEST_PREC)  50.4 us
    all_gather x2, blocking collectives, carried_in(): gathered = jax.tree.map(lambda a: lax.all_gather(a, axis), part)  25.5 us
    psum x1, blocking collectives, per_device(): profile = lax.psum(local_sum, 'path') / (total_paths * date_step)  15 us
    psum x1, blocking collectives, per_device(): lax.psum(LOSS_SHARE * date_step * jnp.sum(own_discount[:, None] * profile...  9.71 us
    unnamed x1, blocking collectives  8.93 us
    all_gather x1, waiting for transfers between devices, carried_in(): gathered = jax.tree.map(lambda a: lax.all_gather(a, axis), part)  6.64 us
    dot_general x1, matrix products, local_walk(): jnp.einsum('ts,jsp->tjp', lower_ones, moves, precision=HIGHEST_PREC)  5.52 us
    while x1, local copies, waits for them, and re-layouts, weigh_dates(): lax.map(lambda block_item: weigh_block(block_item, hazard_scale), blocks)  4.63 us
  transfers between devices with their start and end apart: 1, of which 1 were waited for; matrix products, arithmetic and copies ran while one was open for 2% of the time, Pallas kernels for 0%

commit v1 on v0

--- a/solution.py
+++ b/solution.py
@@ -171,7 +171,12 @@
     discount = jnp.exp(-RATE_DOM * date_step * (jnp.arange(total_dates, dtype=jnp.float32) + 1.0))
     profile = lax.psum(local_sum, "path") / (total_paths * date_step)
     own_discount = lax.dynamic_slice_in_dim(discount, first_date, local_dates, 0)
-    cva = lax.psum(LOSS_SHARE * date_step * jnp.sum(own_discount[:, None] * profile, axis=0), "tm")
+    cva = jnp.sum(
+        lax.all_gather(
+            LOSS_SHARE * date_step * jnp.sum(own_discount[:, None] * profile, axis=0), "tm"
+        ),
+        axis=0,
+    )
     return (profile, cva)
 
 

time: 157 us -> 157 us (level)
    psum x1 -> x0, blocking collectives: 9.71 us -> none  [per_device(): lax.psum(LOSS_SHARE * date_step * jnp.sum(own_discount[:, None] * profile...]
    unnamed x1 -> x2, blocking collectives: 8.93 us -> 18.2 us
    unnamed x23 -> x24, local copies, waits for them, and re-layouts: 3.53 us -> 3.51 us
where the time goes in v1:
time: 157 us
  matrix products  59.4 us (38%)
  blocking collectives  58.3 us (37%)
  between operations  14.9 us (9%)
  local copies, waits for them, and re-layouts  12.4 us (8%)
  waiting for transfers between devices  6.04 us (4%)
  other arithmetic  5.3 us (3%)
    dot_general x8, matrix products, weigh_block(): jnp.einsum('tcj,tjp->tcp', fwd_table, spot, precision=HIGHEST_PREC)  50.3 us
    all_gather x2, blocking collectives, carried_in(): gathered = jax.tree.map(lambda a: lax.all_gather(a, axis), part)  25.1 us
    unnamed x2, blocking collectives  18.2 us
    psum x1, blocking collectives, per_device(): profile = lax.psum(local_sum, 'path') / (total_paths * date_step)  15 us
    all_gather x1, waiting for transfers between devices, carried_in(): gathered = jax.tree.map(lambda a: lax.all_gather(a, axis), part)  6.03 us
    dot_general x1, matrix products, local_walk(): jnp.einsum('ts,jsp->tjp', lower_ones, moves, precision=HIGHEST_PREC)  5.52 us
    while x1, local copies, waits for them, and re-layouts, weigh_dates(): lax.map(lambda block_item: weigh_block(block_item, hazard_scale), blocks)  4.62 us
    unnamed x24, local copies, waits for them, and re-layouts  3.51 us
  transfers between devices with their start and end apart: 1, of which 1 were waited for; matrix products, arithmetic and copies ran while one was open for 2% of the time, Pallas kernels for 0%

profile of v1, /device:TPU:0, one launch (start us, length us, event | category | flops | bytes accessed | tf_op | source)
XLA Modules:
  0.0 156.8 jit_solution(5599662861464383986)
XLA Ops:
  7.2 0.7 broadcast_multiply_fusion.2
  7.9 5.5 %fusion.8 = f32[16,4,16384]{2,0,1:T(8,128)S(1)} fusion(f32[4,16,16384]{2,1,0:T(8,128)} %param.17, f32[4]{0:T(128)S(1)} %get-tuple-element.248, f32[4]{0:T(128)S(1)} %get-tuple-element.251, f32[16,16384]{1,0:T(8,128)} %param.16, f32[4]{0:T(128)} %param.19, f32[4]{0:T(128)S(1)} %get-tuple-element.247), kind=kOutput, calls=%fused_computation.23 | convolution fusion | flops 206569984 | bytes 9437248 | tf_op jit(solution)/shard_map/ts,jsp->tjp/dot_general | solution.py:91
  13.4 1.9 %copy-done = f32[16,4,16384]{2,0,1:T(8,128)} copy-done((f32[16,4,16384]{2,0,1:T(8,128)}, f32[16,4,16384]{2,0,1:T(8,128)S(1)}, u32[]{:S(2)}) %copy-start) | copy-done | bytes 4194328
  15.4 0.2 slice.9
  15.6 0.9 copy.15
  16.6 1.0 convolution_multiply_fusion.1
  17.6 10.5 %all-gather.2 = f32[4,1,16384]{2,1,0:T(1,128)S(1)} all-gather(f32[1,1,16384]{2,1,0:T(1,128)S(1)} %slice_bitcast_fusion), channel_id=1, replica_groups=mesh['path'=8,'tm'=4] {'tm'}, dimensions={0}, use_global_device_ids=true | all-gather | bytes 327680 | tf_op jit(solution)/shard_map/all_gather | solution.py:17
  28.1 0.6 dynamic-slice
  28.7 0.7 dynamic-update-slice
  29.4 8.9 %all-reduce = f32[4]{0:T(128)S(1)} all-reduce(f32[4]{0:T(128)S(1)} %dynamic-update-slice), channel_id=1, replica_groups=mesh['path'=8,'tm'=4] {'tm'}, use_global_device_ids=true, to_apply=%add | all-reduce | flops 4 | bytes 32
  39.7 0.2 fusion.20
  39.9 6.0 %all-gather.5.cloned.1.call-done = f32[4,4,16384]{2,1,0:T(4,128)} async-done(((f32[1,4,16384]{2,1,0:T(4,128)}), f32[4,4,16384]{2,1,0:T(4,128)}) %all-gather.5.cloned.1.call-update) | async-done | bytes 1048592 | tf_op jit(solution)/shard_map/all_gather | solution.py:17
  46.0 2.7 %add_exponential_fusion = f32[16,4,16384]{2,0,1:T(8,128)S(1)} fusion(f32[16,4,16384]{2,0,1:T(8,128)} %copy-done, f32[4,16384]{1,0:T(4,128)S(1)} %get-tuple-element.178), kind=kLoop, calls=%fused_computation.22 | loop fusion | flops 1048576 | bytes 8650752 | tf_op jit(solution)/shard_map/exp | solution.py:106
  48.7 4.6 %copy.18 = f32[16,4,16384]{2,1,0:T(4,128)} copy(f32[16,4,16384]{2,0,1:T(8,128)S(1)} %add_exponential_fusion) | data formatting | bytes 8388608 | tf_op jit(solution)/shard_map/while | solution.py:74
  53.3 0.4 fusion.66
  53.8 14.7 %all-gather = f32[65536]{0:T(1024)S(1)} all-gather(f32[16384]{0:T(1024)S(1)} %broadcast_multiply_fusion), channel_id=2, replica_groups=mesh['path'=8,'tm'=4] {'tm'}, dimensions={0}, use_global_device_ids=true | all-gather | bytes 327680 | tf_op jit(solution)/shard_map/all_gather | solution.py:17
  68.8 2.1 %multiply_subtract_fusion = (f32[16,16384]{1,0:T(8,128)}, f32[16,16384]{1,0:T(8,128)S(1)}) fusion(f32[16,16384]{1,0:T(8,128)S(1)} %convolution_multiply_fusion.1, f32[16384]{0:T(1024)S(1)} %get-tuple-element.179, f32[16]{0:T(128)S(1)} %add_power_fusion, f32[16384]{0:T(1024)S(1)} %get-tuple-element.180), kind=kOutput, calls=%fused_computation.36 | convolution fusion | flops 54526464 | bytes 3276864 | tf_op jit(solution)/shard_map/dot_general | solution.py:102
  70.9 1.8 %reshape.78 = f32[8,2,16384]{2,1,0:T(2,128)S(1)} reshape(f32[16,16384]{1,0:T(8,128)} %get-tuple-element.249) | data formatting | bytes 2097152 | tf_op jit(solution)/shard_map/reshape | solution.py:71
  72.7 0.6 reshape.79
  73.3 51.0 %while.38 = (s32[]{:T(128)}, f32[8,2,32]{2,1,0:T(2,128)S(1)}, f32[8,2,32,4]{2,1,0,3:T(2,128)S(1)}, f32[8,2,4,16384]{3,2,1,0:T(4,128)}, f32[8,2,32]{2,1,0:T(2,128...) while((s32[]{:T(128)}, f32[8,2,32]{2,1,0:T(2,128)S(1)}, ...), condition=%wide.region_7.8_spmd, body=%wide.region_5.7_spmd.sunk | while | flops 57671616 | bytes 1317113 | solution.py:74
  73.4 6.3 %fusion.73 = f32[2,32]{1,0:T(2,128)S(1)} fusion(f32[2,16384]{1,0:T(2,128)S(1)} %get-tuple-element.373, f32[2,16384]{1,0:T(2,128)S(1)} %get-tuple-element.374, f32[32]{0:T(128)S(1)} %bitcast.78, f32[2,32]{1,0:T(2,128)S(1)} %fusion.72, f32[8,2,4,16384]{3,2,1,0:T(4,128)} %get-tuple-element.447, s32[]{:T(128)S(6)} %copy.46, ...), kind=kOutput, calls=%fused_computation.8.clone.1 | convolution fusion | flops 57671616 | bytes 788100 | tf_op jit(solution)/shard_map/while/body/eval_jaxpr/tcj,tjp->tcp/dot_general | solution.py:51
  79.8 6.3 %fusion.73 = f32[2,32]{1,0:T(2,128)S(1)} fusion(f32[2,16384]{1,0:T(2,128)S(1)} %get-tuple-element.373, f32[2,16384]{1,0:T(2,128)S(1)} %get-tuple-element.374, f32[32]{0:T(128)S(1)} %bitcast.78, f32[2,32]{1,0:T(2,128)S(1)} %fusion.72, f32[8,2,4,16384]{3,2,1,0:T(4,128)} %get-tuple-element.447, s32[]{:T(128)S(6)} %copy.46, ...), kind=kOutput, calls=%fused_computation.8.clone.1 | convolution fusion | flops 57671616 | bytes 788100 | tf_op jit(solution)/shard_map/while/body/eval_jaxpr/tcj,tjp->tcp/dot_general | solution.py:51
  86.2 6.3 %fusion.73 = f32[2,32]{1,0:T(2,128)S(1)} fusion(f32[2,16384]{1,0:T(2,128)S(1)} %get-tuple-element.373, f32[2,16384]{1,0:T(2,128)S(1)} %get-tuple-element.374, f32[32]{0:T(128)S(1)} %bitcast.78, f32[2,32]{1,0:T(2,128)S(1)} %fusion.72, f32[8,2,4,16384]{3,2,1,0:T(4,128)} %get-tuple-element.447, s32[]{:T(128)S(6)} %copy.46, ...), kind=kOutput, calls=%fused_computation.8.clone.1 | convolution fusion | flops 57671616 | bytes 788100 | tf_op jit(solution)/shard_map/while/body/eval_jaxpr/tcj,tjp->tcp/dot_general | solution.py:51
  92.5 6.3 %fusion.73 = f32[2,32]{1,0:T(2,128)S(1)} fusion(f32[2,16384]{1,0:T(2,128)S(1)} %get-tuple-element.373, f32[2,16384]{1,0:T(2,128)S(1)} %get-tuple-element.374, f32[32]{0:T(128)S(1)} %bitcast.78, f32[2,32]{1,0:T(2,128)S(1)} %fusion.72, f32[8,2,4,16384]{3,2,1,0:T(4,128)} %get-tuple-element.447, s32[]{:T(128)S(6)} %copy.46, ...), kind=kOutput, calls=%fused_computation.8.clone.1 | convolution fusion | flops 57671616 | bytes 788100 | tf_op jit(solution)/shard_map/while/body/eval_jaxpr/tcj,tjp->tcp/dot_general | solution.py:51
  98.9 6.3 %fusion.73 = f32[2,32]{1,0:T(2,128)S(1)} fusion(f32[2,16384]{1,0:T(2,128)S(1)} %get-tuple-element.373, f32[2,16384]{1,0:T(2,128)S(1)} %get-tuple-element.374, f32[32]{0:T(128)S(1)} %bitcast.78, f32[2,32]{1,0:T(2,128)S(1)} %fusion.72, f32[8,2,4,16384]{3,2,1,0:T(4,128)} %get-tuple-element.447, s32[]{:T(128)S(6)} %copy.46, ...), kind=kOutput, calls=%fused_computation.8.clone.1 | convolution fusion | flops 57671616 | bytes 788100 | tf_op jit(solution)/shard_map/while/body/eval_jaxpr/tcj,tjp->tcp/dot_general | solution.py:51
  105.3 6.3 %fusion.73 = f32[2,32]{1,0:T(2,128)S(1)} fusion(f32[2,16384]{1,0:T(2,128)S(1)} %get-tuple-element.373, f32[2,16384]{1,0:T(2,128)S(1)} %get-tuple-element.374, f32[32]{0:T(128)S(1)} %bitcast.78, f32[2,32]{1,0:T(2,128)S(1)} %fusion.72, f32[8,2,4,16384]{3,2,1,0:T(4,128)} %get-tuple-element.447, s32[]{:T(128)S(6)} %copy.46, ...), kind=kOutput, calls=%fused_computation.8.clone.1 | convolution fusion | flops 57671616 | bytes 788100 | tf_op jit(solution)/shard_map/while/body/eval_jaxpr/tcj,tjp->tcp/dot_general | solution.py:51
  111.6 6.3 %fusion.73 = f32[2,32]{1,0:T(2,128)S(1)} fusion(f32[2,16384]{1,0:T(2,128)S(1)} %get-tuple-element.373, f32[2,16384]{1,0:T(2,128)S(1)} %get-tuple-element.374, f32[32]{0:T(128)S(1)} %bitcast.78, f32[2,32]{1,0:T(2,128)S(1)} %fusion.72, f32[8,2,4,16384]{3,2,1,0:T(4,128)} %get-tuple-element.447, s32[]{:T(128)S(6)} %copy.46, ...), kind=kOutput, calls=%fused_computation.8.clone.1 | convolution fusion | flops 57671616 | bytes 788100 | tf_op jit(solution)/shard_map/while/body/eval_jaxpr/tcj,tjp->tcp/dot_general | solution.py:51
  118.0 6.3 %fusion.73 = f32[2,32]{1,0:T(2,128)S(1)} fusion(f32[2,16384]{1,0:T(2,128)S(1)} %get-tuple-element.373, f32[2,16384]{1,0:T(2,128)S(1)} %get-tuple-element.374, f32[32]{0:T(128)S(1)} %bitcast.78, f32[2,32]{1,0:T(2,128)S(1)} %fusion.72, f32[8,2,4,16384]{3,2,1,0:T(4,128)} %get-tuple-element.447, s32[]{:T(128)S(6)} %copy.46, ...), kind=kOutput, calls=%fused_computation.8.clone.1 | convolution fusion | flops 57671616 | bytes 788100 | tf_op jit(solution)/shard_map/while/body/eval_jaxpr/tcj,tjp->tcp/dot_general | solution.py:51
  124.3 15.0 %psum.7 = f32[16,32]{1,0:T(8,128)S(1)} all-reduce(f32[16,32]{1,0:T(8,128)S(1)} %bitcast.75), channel_id=1, replica_groups=mesh['path'=8,'tm'=4] {'path'}, use_global_device_ids=true, to_apply=%region_8.9 | all-reduce | flops 512 | bytes 4096 | tf_op jit(solution)/shard_map/psum | solution.py:172
  139.4 0.6 multiply_reduce_fusion
  140.1 9.2 %all-reduce.1 = f32[128]{0:T(128)S(1)} all-reduce(f32[128]{0:T(128)S(1)} %multiply_dynamic-update-slice_fusion), channel_id=3, replica_groups=mesh['path'=8,'tm'=4] {'tm'}, use_global_device_ids=true, to_apply=%add.1 | all-reduce | flops 128 | bytes 1024
  149.4 0.5 reduce_sum.40
  (74 shorter events, 1.7 us)
Async XLA Ops:
  7.2 38.7 %all-gather.5.cloned.1.call-start = ((), (), s32[]{:S(2)}) async-start(), calls=%async_computation | async-start | bytes 1310720 | tf_op jit(solution)/shard_map/all_gather | solution.py:17
  7.9 8.7 %copy-start.1 = (f32[16,16384]{1,0:T(8,128)S(1)}, f32[16,16384]{1,0:T(8,128)}, u32[]{:S(2)}) copy-start(f32[16,16384]{1,0:T(8,128)} %param.16) | copy-start | bytes 3145732
  7.9 20.2 %copy-start.8 = (u32[32]{0:T(128)S(1)}, u32[32]{0:T(128)}, u32[]{:S(2)}) copy-start(u32[32]{0:T(128)} %constant.112) | copy-start | bytes 388
  13.4 1.9 %copy-start = (f32[16,4,16384]{2,0,1:T(8,128)}, f32[16,4,16384]{2,0,1:T(8,128)S(1)}, u32[]{:S(2)}) copy-start(f32[16,4,16384]{2,0,1:T(8,128)S(1)} %fusion.8) | copy-start | bytes 12582916
  15.3 23.8 %copy-start.2 = (f32[512]{0:T(512)S(1)}, f32[512]{0:T(512)}, u32[]{:S(2)}) copy-start(f32[512]{0:T(512)} %param.24) | copy-start | bytes 6148
  15.4 23.8 %copy-start.3 = (f32[512]{0:T(512)S(1)}, f32[512]{0:T(512)}, u32[]{:S(2)}) copy-start(f32[512]{0:T(512)} %param.25) | copy-start | bytes 6148
  15.4 24.0 %copy-start.7 = (f32[32]{0:T(128)S(1)}, f32[32]{0:T(128)}, u32[]{:S(2)}) copy-start(f32[32]{0:T(128)} %param.20) | copy-start | bytes 388
  15.4 24.0 %copy-start.4 = (s32[512]{0:T(512)S(1)}, s32[512]{0:T(512)}, u32[]{:S(2)}) copy-start(s32[512]{0:T(512)} %param.22) | copy-start | bytes 6148
  15.4 24.0 %copy-start.5 = (s32[512]{0:T(512)S(1)}, s32[512]{0:T(512)}, u32[]{:S(2)}) copy-start(s32[512]{0:T(512)} %param.23) | copy-start | bytes 6148
  15.4 24.0 %copy-start.6 = (s32[512]{0:T(512)S(1)}, s32[512]{0:T(512)}, u32[]{:S(2)}) copy-start(s32[512]{0:T(512)} %param.21) | copy-start | bytes 6148
Sparse Core Ops, SparseCore 0:
  16.6 29.2 all-gather.4
